TPU v7x, 32 devices: a whole 2x2x4 slice. The times are simulated.
32 devices in a mesh: dp: 16 (over z, x, core), tensor: 2 (over y).
Axes of the slice: x: 2, y: 2, z: 4, core: 2. Of those that a mesh axis runs over, the one named last changes fastest.
Arguments:
- hidden: bfloat16 [5120, 18432], P('dp', 'tensor'), may hold values from -6 to 6
- fixed_down_weight: bfloat16 [18432, 4608], P('tensor', 'dp'), may hold values from -4 to 4
- lowrank_factor_b: bfloat16 [18432, 16], P('tensor'), may hold values from -0.046875 to 0.046875
- lowrank_factor_a: bfloat16 [16, 4608], P(None, 'dp'), may hold values from -1.5 to 1.5
- magnitude: float32 [4608], P('tensor'), may hold values from 0.5 to 2
- cotangent: bfloat16 [5120, 4608], P('dp', 'tensor'), may hold values from -0.083496094 to 0.083496094
Outputs:
- mixed: bfloat16 [5120, 4608], P('dp', 'tensor')
- gradient_column_scale: float32 [4608], P(('tensor', 'dp'))
- gradient_factor_a: float32 [16, 4608], P(None, ('tensor', 'dp'))
- gradient_factor_b: float32 [18432, 16], P(('tensor', 'dp'))
All inputs are finite; a program needn't handle non-finite values.
Results may differ from a plain program's by a relative error of at most 0.0054.
Values may be sent and summed in bfloat16 or wider, within the bound.
A program may use at most 192 MiB of HBM per device.

v0:
```python
import jax
import jax.numpy as jnp
from jax import lax
from jax.sharding import Mesh, PartitionSpec as P

F32, BF16 = (jnp.float32, jnp.bfloat16)


def body(hidden, weight, factor_b, factor_a, magnitude, cotangent, *, n_out, n_in, n_t):
    rows, depth = hidden.shape
    cols = weight.shape[1]
    rank = factor_b.shape[1]
    out_cols = magnitude.shape[0]
    group = 2 * n_in
    dp = ("outer", "mid", "core")
    outer = lax.axis_index("outer")
    place = lax.axis_index("mid") * 2 + lax.axis_index("core")
    own = lax.axis_index("tensor")
    swap_mid = [(i, (i + 1) % n_in) for i in range(n_in)]
    swap_core = [(0, 1), (1, 0)]
    h_mid = lax.ppermute(hidden, "mid", swap_mid)
    w_all = lax.all_gather(weight, "outer", axis=1, tiled=True)
    h_core = lax.ppermute(hidden, "core", swap_core)
    h_both = lax.ppermute(h_mid, "core", swap_core)
    low_part = jnp.dot(hidden, factor_b, preferred_element_type=F32)
    merged = weight.astype(F32) + jnp.dot(factor_b, factor_a, preferred_element_type=F32)
    local_sq = jnp.sum(merged * merged, axis=0)
    low, block_sq = lax.psum((low_part, local_sq), "tensor")
    col_sq = lax.all_gather(block_sq, dp, axis=0, tiled=True)
    full_a = lax.all_gather(factor_a, dp, axis=1, tiled=True)
    norms = jnp.sqrt(lax.dynamic_slice_in_dim(col_sq, own * out_cols, out_cols, 0) + 1e-06)
    scale = magnitude / norms
    low_b = low.astype(BF16)
    own_a = lax.dynamic_slice_in_dim(full_a, own * out_cols, out_cols, 1)
    adapter = jnp.dot(low_b, own_a, preferred_element_type=F32)
    h_all = jnp.zeros((group, rows, depth), BF16)
    for block, flip in ((hidden, 0), (h_core, 1), (h_mid, 2), (h_both, 3)):
        h_all = lax.dynamic_update_slice_in_dim(h_all, block[None], place ^ flip, 0)
    h_rows = h_all.reshape(group * rows, depth)
    cot = cotangent.astype(F32)
    dpre_b = (cot * scale).astype(BF16)
    back_b = lax.psum(jnp.dot(dpre_b, own_a.T, preferred_element_type=F32), "tensor").astype(BF16)
    b_part = jnp.dot(back_b.T, hidden, preferred_element_type=F32)
    a_part = jnp.dot(low_b.T, dpre_b, preferred_element_type=F32)
    n_dp = n_out * group
    parts = jnp.concatenate([x.reshape(rank, n_dp, -1) for x in (a_part, b_part)], axis=2)
    parts = lax.all_to_all(parts.transpose(1, 0, 2), dp, 0, 0, tiled=True)
    sums = jnp.sum(parts, axis=0)
    grad_a = sums[:, : out_cols // n_dp]
    grad_b = sums[:, out_cols // n_dp :].T
    w_all, grad_a, grad_b = lax.optimization_barrier((w_all, grad_a, grad_b))
    per_t = n_out // n_t
    sends = jnp.dot(h_rows, w_all, preferred_element_type=F32).astype(BF16)
    sends = sends.reshape(group, rows, n_t, per_t, cols).transpose(2, 0, 3, 1, 4)
    sends = sends.reshape(n_t * group, per_t, rows, cols)
    got = lax.all_to_all(sends, ("tensor", "mid", "core"), 0, 0, tiled=True)
    got = got.reshape(n_t, group, per_t, rows, cols)
    summed = jnp.sum(got.astype(F32), axis=0).transpose(2, 1, 0, 3).reshape(rows, out_cols)
    pre = summed + adapter
    mixed = (pre * scale).astype(BF16)
    mag_part = jnp.sum(cot * pre, axis=0) / norms
    for axis in ("core", "mid", "outer"):
        mag_part = lax.psum(mag_part, axis)
    at = (outer * group + place) * (out_cols // n_dp)
    grad_scale = lax.dynamic_slice_in_dim(mag_part, at, out_cols // n_dp, 0)
    return (mixed, grad_scale, grad_a, grad_b)


def solution(mesh):
    n_dp, n_t = (mesh.shape["dp"], mesh.shape["tensor"])
    n_in = 2
    n_out = n_dp // (2 * n_in)
    fine = Mesh(mesh.devices.reshape(n_out, n_in, 2, n_t), ("outer", "mid", "core", "tensor"))
    dp = ("outer", "mid", "core")

    def step(*args):
        return body(*args, n_out=n_out, n_in=n_in, n_t=n_t)

    return jax.shard_map(
        step,
        mesh=fine,
        in_specs=(
            P(dp, "tensor"),
            P("tensor", dp),
            P("tensor", None),
            P(None, dp),
            P("tensor"),
            P(dp, "tensor"),
        ),
        out_specs=(
            P(dp, "tensor"),
            P(("tensor",) + dp),
            P(None, ("tensor",) + dp),
            P(("tensor",) + dp, None),
        ),
        check_vma=False,
    )
```

profile of v0, /device:TPU:0, one launch (start us, length us, event | category | flops | bytes accessed | tf_op | source)
XLA Modules:
  0.0 534.6 jit_solution(16286039173848104964)
XLA Ops:
  11.0 144.5 %all-gather = bf16[16,288,16]{1,2,0:T(8,128)(2,1)S(1)} all-gather(bf16[1,288,16]{1,2,0:T(8,128)(2,1)} %bitcast.44), channel_id=1, replica_groups=mesh['outer'=4,'mid'=2,'core'=2,'tensor'=2] {'outer','mid','core'}, dimensions={0}, use_global_device_ids=true | all-gather | bytes 156672 | tf_op jit(solution)/shard_map/all_gather | solution.py:30
  157.0 4.4 fusion.3
  161.4 4.9 psum.43
  166.5 80.5 %all-reduce = f32[4608]{0:T(1024)S(1)} all-reduce(f32[4608]{0:T(1024)S(1)} %dynamic-update-slice), channel_id=1, replica_groups=mesh['outer'=4,'mid'=2,'core'=2,'tensor'=2] {'outer','mid','core'}, use_global_device_ids=true, to_apply=%add | all-reduce | flops 4608 | bytes 36864
  247.7 4.4 fusion.18
  252.1 8.6 %all-reduce.1 = (bf16[320,16]{0,1:T(8,128)(2,1)S(1)}, bf16[320,16]{0,1:T(8,128)(2,1)S(1)}) all-reduce(f32[320,16]{0,1:T(8,128)S(1)} %fusion.4, f32[320,16]{0,1:T(8,128)S(1)} %fusion.18), channel_id=1, replica_groups=mesh['outer'=4,'mid'=2,'core'=2,'tensor'=2] {'tensor'}, use_global_device_ids=true, to_apply=%region_3.0 | all-reduce | flops 10240 | bytes 61440 | tf_op jit(solution)/shard_map/psum | solution.py:42
  261.4 3.7 fusion.19
  266.7 16.8 %all-to-all-start = ((f32[16,16,720]{2,1,0:T(8,128)}), f32[16,16,720]{2,1,0:T(8,128)S(1)}, u32[]{:S(2)}, u32[]{:S(2)}) async-start(f32[16,16,720]{2,1,0:T(8,128)} %maximum_bitcast_fusion), calls=%async_computation | async-start | bytes 1572864 | tf_op jit(solution)/shard_map/all_to_all | solution.py:47
  284.0 8.7 %broadcast_in_dim.17 = bf16[4,320,9216]{2,1,0:T(8,128)(2,1)} broadcast(bf16[]{:T(256)} %constant.14.clone.1), dimensions={} | broadcast | bytes 23592962 | tf_op jit(solution)/shard_map/broadcast_in_dim | solution.py:36
  295.6 25.9 %all-to-all-done = f32[16,16,720]{2,1,0:T(8,128)S(1)} async-done(((f32[16,16,720]{2,1,0:T(8,128)}), f32[16,16,720]{2,1,0:T(8,128)S(1)}, u32[]{:S(2)}, u32[]{:S(2)}) %all-to-all-start) | async-done | bytes 737312 | tf_op jit(solution)/shard_map/all_to_all | solution.py:47
  322.9 5.6 %bitcast_dynamic-update-slice_fusion.2 = bf16[4,320,9216]{2,1,0:T(8,128)(2,1)} fusion(bf16[4,320,9216]{2,1,0:T(8,128)(2,1)} %bitcast_dynamic-update-slice_fusion.3, s32[]{:T(128)S(6)} %select_n.20, bf16[320,9216]{1,0:T(8,128)(2,1)} %collective-permute-done), kind=kLoop, calls=%fused_computation.6 | loop fusion | bytes 11796484 | tf_op jit(solution)/shard_map/dynamic_update_slice | solution.py:38
  328.5 5.6 %bitcast_dynamic-update-slice_fusion.1 = bf16[4,320,9216]{2,1,0:T(8,128)(2,1)} fusion(bf16[4,320,9216]{2,1,0:T(8,128)(2,1)} %bitcast_dynamic-update-slice_fusion.2, s32[]{:T(128)S(6)} %select_n.21, bf16[320,9216]{1,0:T(8,128)(2,1)} %collective-permute-done.1), kind=kLoop, calls=%fused_computation.5 | loop fusion | bytes 11796484 | tf_op jit(solution)/shard_map/dynamic_update_slice | solution.py:38
  334.1 5.6 %bitcast_dynamic-update-slice_fusion = bf16[4,320,9216]{2,1,0:T(8,128)(2,1)} fusion(bf16[4,320,9216]{2,1,0:T(8,128)(2,1)} %bitcast_dynamic-update-slice_fusion.1, s32[]{:T(128)S(6)} %select_n.22, bf16[320,9216]{1,0:T(8,128)(2,1)} %collective-permute-done.2), kind=kLoop, calls=%fused_computation.4 | loop fusion | bytes 11796484 | tf_op jit(solution)/shard_map/dynamic_update_slice | solution.py:38
  339.6 51.8 %all-gather.3.cloned.1.call-done = bf16[9216,1152]{0,1:T(8,128)(2,1)} async-done(((bf16[9216,288]{0,1:T(8,128)(2,1)}), bf16[9216,1152]{0,1:T(8,128)(2,1)}) %all-gather.3.cloned.1.call-update) | async-done | bytes 21233680 | tf_op jit(solution)/shard_map/all_gather | solution.py:22
  391.4 37.6 %convolution_convert_fusion = bf16[1280,1152]{1,0:T(8,128)(2,1)} fusion(bf16[1280,9216]{1,0:T(8,128)(2,1)} %bitcast.39, bf16[9216,1152]{0,1:T(8,128)(2,1)} %all-gather.3.cloned.1.call-done), kind=kOutput, calls=%fused_computation.2 | convolution fusion | flops 27180564480 | bytes 47775744 | tf_op jit(solution)/shard_map/dot_general | solution.py:53
  429.0 3.9 copy.17
  433.0 5.1 reshape.33
  438.1 4.3 copy.18
  442.4 4.5 all-to-all-start.1
  446.9 42.1 %all-to-all-done.1 = bf16[8,2,320,288]{2,3,1,0:T(8,128)(2,1)} async-done(((bf16[8,2,320,288]{2,3,1,0:T(8,128)(2,1)}), bf16[8,2,320,288]{2,3,1,0:T(8,128)(2,1)}, u32[]{:S(2)}, u32[]{:S(2)}) %all-to-all-start.1) | async-done | bytes 2949152 | tf_op jit(solution)/shard_map/all_to_all | solution.py:56
  494.1 3.3 copy.20
  500.7 3.3 psum.45
  504.0 7.1 %psum.46 = f32[2304]{0:T(1024)S(1)} all-reduce(f32[2304]{0:T(1024)S(1)} %psum.45), channel_id=1, replica_groups=mesh['outer'=4,'mid'=2,'core'=2,'tensor'=2] {'mid'}, use_global_device_ids=true, to_apply=%region_8.0 | all-reduce | flops 2304 | bytes 18432 | tf_op jit(solution)/shard_map/psum | solution.py:63
  511.1 16.0 %psum.47 = f32[2304]{0:T(1024)S(1)} all-reduce(f32[2304]{0:T(1024)S(1)} %psum.46), channel_id=1, replica_groups=mesh['outer'=4,'mid'=2,'core'=2,'tensor'=2] {'outer'}, use_global_device_ids=true, to_apply=%region_9.0 | all-reduce | flops 2304 | bytes 18432 | tf_op jit(solution)/shard_map/psum | solution.py:63
  (47 shorter events, 21.5 us)
Async XLA Ops:
  7.2 149.8 %copy-start = (bf16[9216,16]{0,1:T(8,128)(2,1)S(1)}, bf16[9216,16]{0,1:T(8,128)(2,1)}, u32[]{:S(2)}) copy-start(bf16[9216,16]{0,1:T(8,128)(2,1)} %param.8) | copy-start | bytes 884740
  7.2 148.6 %copy-start.5 = (u32[32]{0:T(128)S(1)}, u32[32]{0:T(128)}, u32[]{:S(2)}) copy-start(u32[32]{0:T(128)} %constant.38) | copy-start | bytes 388
  7.2 149.8 %copy-start.3 = (bf16[16,288]{1,0:T(8,128)(2,1)S(1)}, bf16[16,288]{1,0:T(8,128)(2,1)}, u32[]{:S(2)}) copy-start(bf16[16,288]{1,0:T(8,128)(2,1)} %param.9) | copy-start | bytes 27652
  7.2 384.2 %all-gather.3.cloned.1.call-start = ((), (), s32[]{:S(2)}) async-start(), calls=%async_computation.2 | async-start | bytes 26542080 | tf_op jit(solution)/shard_map/all_gather | solution.py:22
  7.9 275.6 %collective-permute-start.1 = (bf16[320,9216]{1,0:T(8,128)(2,1)}, bf16[320,9216]{1,0:T(8,128)(2,1)}, u32[]{:S(2)}, u32[]{:S(2)}) collective-permute-start(bf16[320,9216]{1,0:T(8,128)(2,1)} %param.6), channel_id=1, source_target_pairs={{0,4},{4,0},{1,5},{5,1},{2,6},{6,2},{3,7},{7,3},{8,12},{12,8},{9,1... | collective-permute-start | bytes 17694728 | tf_op jit(solution)/shard_map/ppermute | solution.py:21
  11.0 311.9 %collective-permute-start = (bf16[320,9216]{1,0:T(8,128)(2,1)}, bf16[320,9216]{1,0:T(8,128)(2,1)}, u32[]{:S(2)}, u32[]{:S(2)}) collective-permute-start(bf16[320,9216]{1,0:T(8,128)(2,1)} %param.6), channel_id=1, source_target_pairs={{0,2},{2,0},{1,3},{3,1},{4,6},{6,4},{5,7},{7,5},{8,10},{10,8},{9,1... | collective-permute-start | bytes 17694728 | tf_op jit(solution)/shard_map/ppermute | solution.py:23
  157.0 90.1 %copy-start.4 = (f32[2304]{0:T(1024)S(1)}, f32[2304]{0:T(1024)}, u32[]{:S(2)}) copy-start(f32[2304]{0:T(1024)} %param.10) | copy-start | bytes 27652
  157.0 90.2 %copy-start.2 = (bf16[320,2304]{1,0:T(8,128)(2,1)S(1)}, bf16[320,2304]{1,0:T(8,128)(2,1)}, u32[]{:S(2)}) copy-start(bf16[320,2304]{1,0:T(8,128)(2,1)} %param.11) | copy-start | bytes 4423684
  266.7 54.8 %all-to-all-start = ((f32[16,16,720]{2,1,0:T(8,128)}), f32[16,16,720]{2,1,0:T(8,128)S(1)}, u32[]{:S(2)}, u32[]{:S(2)}) async-start(f32[16,16,720]{2,1,0:T(8,128)} %maximum_bitcast_fusion), calls=%async_computation | async-start | bytes 1572864 | tf_op jit(solution)/shard_map/all_to_all | solution.py:47
  283.5 9.2 %slice-start = ((s8[5898240]{0:T(1024)(128)(4,1)}), s8[1703936]{0:T(1024)(128)(4,1)S(1)}, s32[]{:S(2)}) async-start(s8[5898240]{0:T(1024)(128)(4,1)} %bitcast.37), calls=%async_computation.3 | async-start | bytes 3407872
  283.5 9.2 %slice-start.1 = ((s8[5898240]{0:T(1024)(128)(4,1)}), s8[4194304]{0:T(1024)(128)(4,1)S(1)}, s32[]{:S(2)}) async-start(s8[5898240]{0:T(1024)(128)(4,1)} %bitcast.37), calls=%async_computation.4 | async-start | bytes 8388608
  283.5 50.5 %collective-permute-start.2 = (bf16[320,9216]{1,0:T(8,128)(2,1)}, bf16[320,9216]{1,0:T(8,128)(2,1)}, u32[]{:S(2)}, u32[]{:S(2)}) collective-permute-start(bf16[320,9216]{1,0:T(8,128)(2,1)} %collective-permute-done.1), channel_id=1, source_target_pairs={{0,2},{2,0},{1,3},{3,1},{4,6},{6,4},{5,7},{7,5},{8,10},{10,8},{9,1... | collective-permute-start | bytes 17694728 | tf_op jit(solution)/shard_map/ppermute | solution.py:24
  442.4 46.6 %all-to-all-start.1 = ((bf16[8,2,320,288]{2,3,1,0:T(8,128)(2,1)}), bf16[8,2,320,288]{2,3,1,0:T(8,128)(2,1)}, u32[]{:S(2)}, u32[]{:S(2)}) async-start(bf16[8,2,320,288]{2,3,1,0:T(8,128)(2,1)} %bitcast.40), calls=%async_computation.1 | async-start | bytes 7077888 | tf_op jit(solution)/shard_map/all_to_all | solution.py:56
  494.1 33.6 %copy-start.1 = (bf16[9216,16]{0,1:T(8,128)(2,1)S(1)}, bf16[9216,16]{0,1:T(8,128)(2,1)}, u32[]{:S(2)}) copy-start(bf16[9216,16]{0,1:T(8,128)(2,1)} %param.8) | copy-start | bytes 884740
Sparse Core Ops, SparseCore 0:
  9.6 381.7 all-gather.2
where the time goes:
time: 535 us
  blocking collectives  265 us (50%)
  waiting for transfers between devices  120 us (22%)
  matrix products  54.2 us (10%)
  local copies, waits for them, and re-layouts  50.8 us (9%)
  starting transfers between devices  24.8 us (5%)
  between operations  14.9 us (3%)
    all_gather x1, blocking collectives, body(): full_a = lax.all_gather(factor_a, dp, axis=1, tiled=True)  145 us
    unnamed x1, blocking collectives  80.5 us
    all_gather x1, waiting for transfers between devices, body(): w_all = lax.all_gather(weight, 'outer', axis=1, tiled=True)  51.8 us
    all_to_all x1, waiting for transfers between devices, body(): got = lax.all_to_all(sends, ('tensor', 'mid', 'core'), 0, 0, tiled=True)  42.1 us
    dot_general x1, matrix products, body(): sends = jnp.dot(h_rows, w_all, preferred_element_type=F32).astype(BF16)  37.6 us
    psum x3, blocking collectives, body(): mag_part = lax.psum(mag_part, axis)  26.4 us
    all_to_all x1, waiting for transfers between devices, body(): parts = lax.all_to_all(parts.transpose(1, 0, 2), dp, 0, 0, tiled=True)  25.9 us
    dynamic_update_slice x4, local copies, waits for them, and re-layouts, body(): h_all = lax.dynamic_update_slice_in_dim(h_all, block[None], place ^ flip, 0)  19.6 us
  transfers between devices with their start and end apart: 6, of which 3 were waited for; matrix products, arithmetic and copies ran while one was open for 9% of the time, Pallas kernels for 0%

commit v1 on v0

--- a/solution.py
+++ b/solution.py
@@ -4,6 +4,12 @@
 from jax.sharding import Mesh, PartitionSpec as P
 
 F32, BF16 = (jnp.float32, jnp.bfloat16)
+
+
+def gather_blocks(x, name, dim):
+    parts = lax.all_gather(x, name, axis=0, tiled=False)
+    whole = jnp.concatenate(parts, axis=dim)
+    return whole
 
 
 def body(hidden, weight, factor_b, factor_a, magnitude, cotangent, *, n_out, n_in, n_t):
@@ -19,7 +25,7 @@
     swap_mid = [(i, (i + 1) % n_in) for i in range(n_in)]
     swap_core = [(0, 1), (1, 0)]
     h_mid = lax.ppermute(hidden, "mid", swap_mid)
-    w_all = lax.all_gather(weight, "outer", axis=1, tiled=True)
+    w_all = gather_blocks(weight, "outer", 1)
     h_core = lax.ppermute(hidden, "core", swap_core)
     h_both = lax.ppermute(h_mid, "core", swap_core)
     low_part = jnp.dot(hidden, factor_b, preferred_element_type=F32)

time: 535 us -> 587 us (1.097)
  local copies, waits for them, and re-layouts: 50.8 us -> 101 us
    all_gather x0 -> x1, local copies, waits for them, and re-layouts: none -> 33.4 us  [gather_blocks(): parts = lax.all_gather(x, name, axis=0, tiled=False)]
    reshape x0 -> x1, local copies, waits for them, and re-layouts: none -> 17.1 us  [gather_blocks(): whole = jnp.concatenate(parts, axis=dim)]
  transfers between devices with their start and end apart: 6 -> 6, of which waited for: 3 -> 3; matrix products, arithmetic and copies ran while one was open for 9% -> 8% of each run, Pallas kernels for 0% -> 0%
where the time goes in v1:
time: 587 us; the launch traced here: 585 us
  blocking collectives  265 us (45%)
  waiting for transfers between devices  120 us (20%)
  local copies, waits for them, and re-layouts  101 us (17%)
  matrix products  54.2 us (9%)
  starting transfers between devices  25 us (4%)
  between operations  14.9 us (3%)
    all_gather x1, blocking collectives, body(): full_a = lax.all_gather(factor_a, dp, axis=1, tiled=True)  145 us
    unnamed x1, blocking collectives  80.5 us
    all_gather x1, waiting for transfers between devices, gather_blocks(): parts = lax.all_gather(x, name, axis=0, tiled=False)  51.8 us
    all_to_all x1, waiting for transfers between devices, body(): got = lax.all_to_all(sends, ('tensor', 'mid', 'core'), 0, 0, tiled=True)  41.8 us
    dot_general x1, matrix products, body(): sends = jnp.dot(h_rows, w_all, preferred_element_type=F32).astype(BF16)  37.6 us
    all_gather x1, local copies, waits for them, and re-layouts, gather_blocks(): parts = lax.all_gather(x, name, axis=0, tiled=False)  33.4 us
    psum x3, blocking collectives, body(): mag_part = lax.psum(mag_part, axis)  26.3 us
    all_to_all x1, waiting for transfers between devices, body(): parts = lax.all_to_all(parts.transpose(1, 0, 2), dp, 0, 0, tiled=True)  25.9 us
  transfers between devices with their start and end apart: 6, of which 3 were waited for; matrix products, arithmetic and copies ran while one was open for 8% of the time, Pallas kernels for 0%

profile of v1, /device:TPU:0, one launch (start us, length us, event | category | flops | bytes accessed | tf_op | source)
XLA Modules:
  0.0 584.9 jit_solution(12785664437475302987)
XLA Ops:
  11.0 144.5 %all-gather.1 = bf16[16,288,16]{1,2,0:T(8,128)(2,1)S(1)} all-gather(bf16[1,288,16]{1,2,0:T(8,128)(2,1)} %bitcast.50), channel_id=1, replica_groups=mesh['outer'=4,'mid'=2,'core'=2,'tensor'=2] {'outer','mid','core'}, dimensions={0}, use_global_device_ids=true | all-gather | bytes 156672 | tf_op jit(solution)/shard_map/all_gather | solution.py:36
  157.0 4.4 fusion.3
  161.4 4.9 psum.43
  166.5 80.5 %all-reduce = f32[4608]{0:T(1024)S(1)} all-reduce(f32[4608]{0:T(1024)S(1)} %dynamic-update-slice), channel_id=1, replica_groups=mesh['outer'=4,'mid'=2,'core'=2,'tensor'=2] {'outer','mid','core'}, use_global_device_ids=true, to_apply=%add | all-reduce | flops 4608 | bytes 36864
  247.6 4.4 fusion.18
  252.0 8.6 %all-reduce.1 = (bf16[320,16]{0,1:T(8,128)(2,1)S(1)}, bf16[320,16]{0,1:T(8,128)(2,1)S(1)}) all-reduce(f32[320,16]{0,1:T(8,128)S(1)} %fusion.4, f32[320,16]{0,1:T(8,128)S(1)} %fusion.18), channel_id=1, replica_groups=mesh['outer'=4,'mid'=2,'core'=2,'tensor'=2] {'tensor'}, use_global_device_ids=true, to_apply=%region_3.0 | all-reduce | flops 10240 | bytes 61440 | tf_op jit(solution)/shard_map/psum | solution.py:48
  260.6 3.7 fusion.19
  266.6 16.8 %all-to-all-start = ((f32[16,16,720]{2,1,0:T(8,128)}), f32[16,16,720]{2,1,0:T(8,128)S(1)}, u32[]{:S(2)}, u32[]{:S(2)}) async-start(f32[16,16,720]{2,1,0:T(8,128)} %maximum_bitcast_fusion), calls=%async_computation | async-start | bytes 1572864 | tf_op jit(solution)/shard_map/all_to_all | solution.py:53
  283.9 8.7 %broadcast_in_dim.17 = bf16[4,320,9216]{2,1,0:T(8,128)(2,1)} broadcast(bf16[]{:T(256)} %constant.14.clone.1), dimensions={} | broadcast | bytes 23592962 | tf_op jit(solution)/shard_map/broadcast_in_dim | solution.py:42
  295.5 25.9 %all-to-all-done = f32[16,16,720]{2,1,0:T(8,128)S(1)} async-done(((f32[16,16,720]{2,1,0:T(8,128)}), f32[16,16,720]{2,1,0:T(8,128)S(1)}, u32[]{:S(2)}, u32[]{:S(2)}) %all-to-all-start) | async-done | bytes 737312 | tf_op jit(solution)/shard_map/all_to_all | solution.py:53
  322.8 5.6 bitcast_dynamic-update-slice_fusion.2
  328.4 5.6 bitcast_dynamic-update-slice_fusion.1
  334.0 5.6 bitcast_dynamic-update-slice_fusion
  339.6 51.8 %all-gather.4.cloned.1.call-done = bf16[36864,288]{0,1:T(8,128)(2,1)} async-done(((bf16[9216,288]{0,1:T(8,128)(2,1)}), bf16[36864,288]{0,1:T(8,128)(2,1)}) %all-gather.4.cloned.1.call-update) | async-done | bytes 21233680 | tf_op jit(solution)/shard_map/all_gather | solution.py:10
  391.4 33.4 %reshape.45 = bf16[4,9216,288]{1,0,2:T(4,128)(2,1)} reshape(bf16[36864,288]{0,1:T(8,128)(2,1)} %all-gather.4.cloned.1.call-done) | data formatting | bytes 42467328 | tf_op jit(solution)/shard_map/all_gather | solution.py:10
  424.7 17.1 %copy.19 = bf16[9216,4,288]{0,2,1:T(8,128)(2,1)} copy(bf16[9216,4,288]{0,1,2:T(4,128)(2,1)} %bitcast.43) | data formatting | bytes 42467328 | tf_op jit(solution)/shard_map/reshape | solution.py:11
  441.8 37.6 %convolution_convert_fusion = bf16[1280,1152]{1,0:T(8,128)(2,1)} fusion(bf16[1280,9216]{1,0:T(8,128)(2,1)} %bitcast.44, bf16[9216,1152]{0,1:T(8,128)(2,1)} %bitcast.45), kind=kOutput, calls=%fused_computation.2 | convolution fusion | flops 27180564480 | bytes 47775744 | tf_op jit(solution)/shard_map/dot_general | solution.py:59
  479.4 3.9 copy.23
  483.4 5.1 reshape.41
  488.5 4.3 copy.24
  492.8 4.7 all-to-all-start.1
  497.5 41.8 %all-to-all-done.1 = bf16[8,2,320,288]{2,3,1,0:T(8,128)(2,1)} async-done(((bf16[8,2,320,288]{2,3,1,0:T(8,128)(2,1)}), bf16[8,2,320,288]{2,3,1,0:T(8,128)(2,1)}, u32[]{:S(2)}, u32[]{:S(2)}) %all-to-all-start.1) | async-done | bytes 2949152 | tf_op jit(solution)/shard_map/all_to_all | solution.py:62
  554.4 7.1 %psum.46 = f32[2304]{0:T(1024)S(1)} all-reduce(f32[2304]{0:T(1024)S(1)} %psum.45), channel_id=1, replica_groups=mesh['outer'=4,'mid'=2,'core'=2,'tensor'=2] {'mid'}, use_global_device_ids=true, to_apply=%region_8.0 | all-reduce | flops 2304 | bytes 18432 | tf_op jit(solution)/shard_map/psum | solution.py:69
  561.5 16.0 %psum.47 = f32[2304]{0:T(1024)S(1)} all-reduce(f32[2304]{0:T(1024)S(1)} %psum.46), channel_id=1, replica_groups=mesh['outer'=4,'mid'=2,'core'=2,'tensor'=2] {'outer'}, use_global_device_ids=true, to_apply=%region_9.0 | all-reduce | flops 2304 | bytes 18432 | tf_op jit(solution)/shard_map/psum | solution.py:69
  (49 shorter events, 28.1 us)
Async XLA Ops:
  7.2 149.8 %copy-start = (bf16[9216,16]{0,1:T(8,128)(2,1)S(1)}, bf16[9216,16]{0,1:T(8,128)(2,1)}, u32[]{:S(2)}) copy-start(bf16[9216,16]{0,1:T(8,128)(2,1)} %param.8) | copy-start | bytes 884740
  7.2 148.6 %copy-start.5 = (u32[32]{0:T(128)S(1)}, u32[32]{0:T(128)}, u32[]{:S(2)}) copy-start(u32[32]{0:T(128)} %constant.38) | copy-start | bytes 388
  7.2 149.8 %copy-start.3 = (bf16[16,288]{1,0:T(8,128)(2,1)S(1)}, bf16[16,288]{1,0:T(8,128)(2,1)}, u32[]{:S(2)}) copy-start(bf16[16,288]{1,0:T(8,128)(2,1)} %param.9) | copy-start | bytes 27652
  7.2 384.2 %all-gather.4.cloned.1.call-start = ((), (), s32[]{:S(2)}) async-start(), calls=%async_computation.2 | async-start | bytes 26542080 | tf_op jit(solution)/shard_map/all_gather | solution.py:10
  7.9 275.5 %collective-permute-start.1 = (bf16[320,9216]{1,0:T(8,128)(2,1)}, bf16[320,9216]{1,0:T(8,128)(2,1)}, u32[]{:S(2)}, u32[]{:S(2)}) collective-permute-start(bf16[320,9216]{1,0:T(8,128)(2,1)} %param.6), channel_id=1, source_target_pairs={{0,4},{4,0},{1,5},{5,1},{2,6},{6,2},{3,7},{7,3},{8,12},{12,8},{9,1... | collective-permute-start | bytes 17694728 | tf_op jit(solution)/shard_map/ppermute | solution.py:27
  11.0 311.8 %collective-permute-start = (bf16[320,9216]{1,0:T(8,128)(2,1)}, bf16[320,9216]{1,0:T(8,128)(2,1)}, u32[]{:S(2)}, u32[]{:S(2)}) collective-permute-start(bf16[320,9216]{1,0:T(8,128)(2,1)} %param.6), channel_id=1, source_target_pairs={{0,2},{2,0},{1,3},{3,1},{4,6},{6,4},{5,7},{7,5},{8,10},{10,8},{9,1... | collective-permute-start | bytes 17694728 | tf_op jit(solution)/shard_map/ppermute | solution.py:29
  157.0 90.0 %copy-start.4 = (f32[2304]{0:T(1024)S(1)}, f32[2304]{0:T(1024)}, u32[]{:S(2)}) copy-start(f32[2304]{0:T(1024)} %param.10) | copy-start | bytes 27652
  157.0 90.1 %copy-start.2 = (bf16[320,2304]{1,0:T(8,128)(2,1)S(1)}, bf16[320,2304]{1,0:T(8,128)(2,1)}, u32[]{:S(2)}) copy-start(bf16[320,2304]{1,0:T(8,128)(2,1)} %param.11) | copy-start | bytes 4423684
  266.6 54.8 %all-to-all-start = ((f32[16,16,720]{2,1,0:T(8,128)}), f32[16,16,720]{2,1,0:T(8,128)S(1)}, u32[]{:S(2)}, u32[]{:S(2)}) async-start(f32[16,16,720]{2,1,0:T(8,128)} %maximum_bitcast_fusion), calls=%async_computation | async-start | bytes 1572864 | tf_op jit(solution)/shard_map/all_to_all | solution.py:53
  283.4 9.2 %slice-start = ((s8[5898240]{0:T(1024)(128)(4,1)}), s8[1703936]{0:T(1024)(128)(4,1)S(1)}, s32[]{:S(2)}) async-start(s8[5898240]{0:T(1024)(128)(4,1)} %bitcast.41), calls=%async_computation.3 | async-start | bytes 3407872
  283.4 9.2 %slice-start.1 = ((s8[5898240]{0:T(1024)(128)(4,1)}), s8[4194304]{0:T(1024)(128)(4,1)S(1)}, s32[]{:S(2)}) async-start(s8[5898240]{0:T(1024)(128)(4,1)} %bitcast.41), calls=%async_computation.4 | async-start | bytes 8388608
  283.4 50.6 %collective-permute-start.2 = (bf16[320,9216]{1,0:T(8,128)(2,1)}, bf16[320,9216]{1,0:T(8,128)(2,1)}, u32[]{:S(2)}, u32[]{:S(2)}) collective-permute-start(bf16[320,9216]{1,0:T(8,128)(2,1)} %collective-permute-done.1), channel_id=1, source_target_pairs={{0,2},{2,0},{1,3},{3,1},{4,6},{6,4},{5,7},{7,5},{8,10},{10,8},{9,1... | collective-permute-start | bytes 17694728 | tf_op jit(solution)/shard_map/ppermute | solution.py:30
  492.8 46.6 %all-to-all-start.1 = ((bf16[8,2,320,288]{2,3,1,0:T(8,128)(2,1)}), bf16[8,2,320,288]{2,3,1,0:T(8,128)(2,1)}, u32[]{:S(2)}, u32[]{:S(2)}) async-start(bf16[8,2,320,288]{2,3,1,0:T(8,128)(2,1)} %bitcast.46), calls=%async_computation.1 | async-start | bytes 7077888 | tf_op jit(solution)/shard_map/all_to_all | solution.py:62
  544.5 33.6 %copy-start.1 = (bf16[9216,16]{0,1:T(8,128)(2,1)S(1)}, bf16[9216,16]{0,1:T(8,128)(2,1)}, u32[]{:S(2)}) copy-start(bf16[9216,16]{0,1:T(8,128)(2,1)} %param.8) | copy-start | bytes 884740
Sparse Core Ops, SparseCore 0:
  9.6 381.7 all-gather.3
